TPU v7x, 32 devices: a whole 2x2x4 slice. The times are simulated.
32 devices in a mesh: gx: 2 (over core), gy: 4 (over y, x), gz: 4 (over z).
Axes of the slice: x: 2, y: 2, z: 4, core: 2. Of those that a mesh axis runs over, the one named last changes fastest.
Arguments:
- queries: bfloat16 [128, 32, 128], P(None, 'gy'), may hold values from -6 to 6
- passages: bfloat16 [1024, 256, 128], P('gx', 'gz'), may hold values from -0.5 to 0.5
- passage_len: int32 [1024], P('gx'), may hold values from 32 to 256
- query_len: int32 [128], replicated, may hold values from 8 to 32
Outputs:
- log_probs: float32 [128, 1024], P(None, ('gx', 'gz'))
All inputs are finite; a program needn't handle non-finite values.
Results may differ from a plain program's by a relative error of at most 0.0003.
Values sent between devices are 32-bit elements; how exact they have to be, the bound alone decides.
A program may use at most 64 MiB of HBM per device.

v0:
```python
import functools

import jax
import jax.numpy as jnp
from jax import lax
from jax.experimental import pallas as pl
from jax.experimental.pallas import tpu as pltpu
from jax.sharding import PartitionSpec as P

masked_low = -1e30
MESH = pl.DeviceIdType.MESH
HOP_LAG = 3
PEER_LAG = 3
PER_CHUNK = 16
PARTS = 1


def kernel(
    sizes,
    queries_in,
    lengths_in,
    query_len_in,
    passages,
    out,
    queries,
    lengths,
    query_len,
    x,
    masked_x,
    wide_queries,
    query_columns,
    limits,
    own_low,
    own_high,
    got_low,
    got_high,
    partials,
    forward,
    total,
    stats,
    small_sem,
    load_sem,
    z_send,
    low_recv,
    high_recv,
    peer_send,
    peer_recv,
    forward_send,
    forward_recv,
    stat_send,
    stat_recv,
):
    nx, ny, nz = sizes
    gx, gy, gz = (lax.axis_index(name) for name in ("gx", "gy", "gz"))
    passage_count, token_count, width = x.shape
    query_count, query_rows, _ = queries.shape
    slots, per_chunk, row_count = own_low.shape
    chunks = slots - 1
    part_rows = per_chunk // PARTS
    half_blocks = nz // 2
    per_block = chunks // half_blocks
    block_rows = passage_count // nz

    def low_start(c):
        return (half_blocks - 1 - c // per_block) * block_rows + (c % per_block) * per_chunk

    def high_start(c):
        return half_blocks * block_rows + c * per_chunk

    barrier = pltpu.get_barrier_semaphore()
    for axis, place, count in (("gx", gx, nx), ("gy", gy, ny), ("gz", gz, nz)):
        for turn in range(1, count):
            pl.semaphore_signal(
                barrier,
                inc=1,
                device_id={axis: lax.rem(place + turn, count)},
                device_id_type=MESH,
            )

    small = [
        pltpu.make_async_copy(source, target, small_sem.at[index])
        for index, (source, target) in enumerate(
            ((queries_in, queries), (lengths_in, lengths), (query_len_in, query_len))
        )
    ]
    for copy in small:
        copy.start()

    def load(start, index):
        rows = pl.ds(start, per_chunk)
        return pltpu.make_async_copy(passages.at[rows], x.at[rows], load_sem.at[index])

    def start_loads(c, carry):
        load(low_start(c), c).start()
        load(high_start(c), chunks + c).start()
        return carry

    lax.fori_loop(0, chunks, start_loads, 0)

    for copy in small:
        copy.wait()

    wide_queries[...] = queries[...].astype(jnp.float32).reshape(row_count, width)
    for i in range(query_rows):
        tile = wide_queries[pl.ds(i, query_count, stride=query_rows), :]
        query_columns[:, i * query_count : (i + 1) * query_count] = tile.T.astype(jnp.bfloat16)

    first_token = (gz * token_count).astype(jnp.float32)
    for b in range(passage_count // 128):
        row = lengths[b : b + 1, :].astype(jnp.float32) - first_token
        limits[b * 128 : (b + 1) * 128, :] = jnp.broadcast_to(row, (128, 128)).T

    token_ids = lax.broadcasted_iota(jnp.int32, (token_count, width), 0).astype(jnp.float32)
    tile_columns = 256

    def compute(c):
        starts = (low_start(c), high_start(c))
        limit = []
        for half, start in enumerate(starts):
            for p in range(per_chunk):
                tokens = x[start + p].astype(jnp.float32)
                usable = token_ids < limits[pl.ds(start + p, 1), :]
                tokens = jnp.where(usable, tokens, tokens[0:1, :])
                row = (half * per_chunk + p) * token_count
                masked_x[row : row + token_count, :] = tokens.astype(jnp.bfloat16)
            limit.append(limits[pl.ds(start, per_chunk), :])
        limit = jnp.concatenate(limit, axis=0)
        any_used = jnp.concatenate([limit] * (tile_columns // 128), axis=1) > 0.0
        for t in range(row_count // tile_columns):
            columns = slice(t * tile_columns, (t + 1) * tile_columns)
            scores = jnp.dot(
                masked_x[...], query_columns[:, columns], preferred_element_type=jnp.float32
            )
            best = jnp.max(scores.reshape(2 * per_chunk, token_count, tile_columns), axis=1)
            best = jnp.where(any_used, best, masked_low)
            own_low[c, :, columns] = best[:per_chunk]
            own_high[c, :, columns] = best[per_chunk:]

    class Flow:
        def __init__(self, own, got, recv, send_index, hops, is_last, target):
            self.own, self.got, self.recv, self.send_index = own, got, recv, send_index
            self.is_first, self.is_last, self.target = hops == 0, is_last, target
            self.lag = HOP_LAG * hops

        def copy(self, source, c, part):
            rows = pl.ds(part * part_rows, part_rows)
            return pltpu.make_async_remote_copy(
                src_ref=source.at[c, rows],
                dst_ref=self.got.at[c, rows],
                send_sem=z_send.at[self.send_index],
                recv_sem=self.recv.at[c, part],
                device_id={"gz": self.target},
                device_id_type=MESH,
            )

        def merge(self, c, rows):
            self.got[c, rows] = jnp.maximum(self.got[c, rows], self.own[c, rows])

        def pass_on(self, c, part):
            @pl.when(jnp.logical_not(self.is_last))
            def _():
                self.copy(self.got, c, part).start()

            @pl.when(self.is_last)
            def _():
                finalise(self.got, c, part)

    first, last = gz == 0, gz == nz - 1
    low = Flow(own_low, got_low, low_recv, 0, nz - 1 - gz, first, lax.rem(gz + nz - 1, nz))
    high = Flow(own_high, got_high, high_recv, 1, gz, last, lax.rem(gz + 1, nz))
    flows = (low, high)

    def peer_copy(turn, slot, block, where):
        return pltpu.make_async_remote_copy(
            src_ref=partials.at[(slot, *where)],
            dst_ref=partials.at[(slot, *where)],
            send_sem=peer_send.at[turn],
            recv_sem=peer_recv.at[slot, block],
            device_id={"gy": lax.rem(gy + turn, ny)},
            device_id_type=MESH,
        )

    def finalise(merged, c, part):
        rows = pl.ds(part * part_rows, part_rows)
        counted = query_len[...] - gy * query_rows
        so_far = jnp.zeros((part_rows, query_count), jnp.float32)
        for i in range(query_rows):
            values = merged[c, rows, i * query_count : (i + 1) * query_count]
            so_far = so_far + jnp.where(counted > i, values, 0.0)
        partials[gy, c, rows] = so_far
        for turn in range(1, ny):
            peer_copy(turn, gy, c // per_block, (c, rows)).start()

    def block_total(block):
        where = pl.ds(block * per_block, per_block)
        for turn in range(1, ny):
            slot = lax.rem(gy + turn, ny)
            peer_copy(turn, slot, block, (where,)).wait_recv()
        summed = partials[0, where]
        for slot in range(1, ny):
            summed = summed + partials[slot, where]
        return summed.reshape(block_rows, query_count)

    def forward_copy(block):
        target = jnp.where(gz == 0, half_blocks - 1 - block, half_blocks + block)
        return pltpu.make_async_remote_copy(
            src_ref=forward.at[block],
            dst_ref=total,
            send_sem=forward_send.at[block],
            recv_sem=forward_recv,
            device_id={"gz": target},
            device_id_type=MESH,
        )

    at_end = (gz == 0) | (gz == nz - 1)

    def forward_ready_block(s):
        ready = s - HOP_LAG * (nz - 1) - PEER_LAG
        for block in range(half_blocks - 1):
            @pl.when(at_end & (ready == (block + 1) * per_block - 1))
            def _():
                forward[block] = block_total(block)
                forward_copy(block).start()

    def step(s, carry):
        for flow in flows:
            c = s - flow.lag

            @pl.when(jnp.logical_not(flow.is_first) & (c >= 0))
            def _():
                for part in range(PARTS):
                    flow.copy(flow.got, c, part).wait_recv()
                    flow.merge(c, pl.ds(part * part_rows, part_rows))
                    flow.pass_on(c, part)

        load(low_start(s), s).wait()
        load(high_start(s), chunks + s).wait()
        compute(s)

        for flow in flows:
            @pl.when(flow.is_first)
            def _():
                for part in range(PARTS):
                    flow.copy(flow.own, s, part).start()

        forward_ready_block(s)
        return carry

    pl.semaphore_wait(barrier, nx + ny + nz - 3)
    lax.fori_loop(0, chunks, step, 0)

    def drain(s, carry):
        for flow in flows:
            c = s - flow.lag

            @pl.when(jnp.logical_not(flow.is_first) & (c >= 0) & (c < chunks))
            def _():
                for part in range(PARTS):
                    flow.copy(flow.got, c, part).wait_recv()
                    flow.merge(c, pl.ds(part * part_rows, part_rows))
                    flow.pass_on(c, part)

        forward_ready_block(s)
        return carry

    lax.fori_loop(chunks, chunks + HOP_LAG * (nz - 1), drain, 0)

    @pl.when(at_end)
    def _():
        total[...] = block_total(half_blocks - 1)

    @pl.when(jnp.logical_not(at_end))
    def _():
        forward_copy(0).wait_recv()

    scores = total[...]
    row_ids = lax.broadcasted_iota(jnp.int32, stats.shape[1:], 0)

    def stat_copy(axis, base, place, count, slot, turn):
        return pltpu.make_async_remote_copy(
            src_ref=stats.at[base + slot],
            dst_ref=stats.at[base + slot],
            send_sem=stat_send.at[base + turn],
            recv_sem=stat_recv.at[base + slot],
            device_id={axis: lax.rem(place + turn, count)},
            device_id_type=MESH,
        )

    def join(axis, base, place, count, top, summed):
        stats[base + place] = jnp.where(row_ids == 0, top, summed)
        for turn in range(1, count):
            stat_copy(axis, base, place, count, place, turn).start()
        for turn in range(1, count):
            slot = lax.rem(place + turn, count)
            stat_copy(axis, base, place, count, slot, turn).wait_recv()
        tops = stats[base : base + count, 0, :]
        sums = stats[base : base + count, 1, :]
        highest = jnp.max(tops, axis=0, keepdims=True)
        return highest, jnp.sum(sums * jnp.exp(tops - highest), axis=0, keepdims=True)

    top = jnp.max(scores, axis=0, keepdims=True)
    summed = jnp.sum(jnp.exp(scores - top), axis=0, keepdims=True)
    top, summed = join("gx", 0, gx, nx, top, summed)
    top, summed = join("gz", nx, gz, nz, top, summed)
    out[...] = (scores - (top + jnp.log(summed))).T

    for flow in flows:
        @pl.when(jnp.logical_not(flow.is_last))
        def _():
            whole = pl.ds(0, chunks)
            pltpu.make_async_remote_copy(
                src_ref=flow.got.at[whole],
                dst_ref=flow.got.at[whole],
                send_sem=z_send.at[flow.send_index],
                recv_sem=flow.recv.at[0, 0],
                device_id={"gz": flow.target},
                device_id_type=MESH,
            ).wait_send()

    @pl.when(at_end)
    def _():
        for turn in range(1, ny):
            peer_copy(turn, gy, 0, (pl.ds(0, chunks),)).wait_send()
        for block in range(half_blocks - 1):
            forward_copy(block).wait_send()

    for axis, base, place, count in (("gx", 0, gx, nx), ("gz", nx, gz, nz)):
        for turn in range(1, count):
            stat_copy(axis, base, place, count, place, turn).wait_send()


def shards(sizes, queries, passages, passage_len, query_len):
    nx, ny, nz = sizes
    query_count, query_rows, width = queries.shape
    passage_count, token_count, _ = passages.shape
    row_count = query_count * query_rows
    block_rows = passage_count // nz
    per_chunk = PER_CHUNK
    chunks = passage_count // 2 // per_chunk
    half_blocks = nz // 2
    maxima = pltpu.VMEM((chunks + 1, per_chunk, row_count), jnp.float32)
    dma = pltpu.SemaphoreType.DMA
    anywhere = pl.BlockSpec(memory_space=pltpu.HBM)
    return pl.pallas_call(
        functools.partial(kernel, sizes),
        out_shape=jax.ShapeDtypeStruct((query_count, block_rows), jnp.float32),
        in_specs=[anywhere] * 4,
        out_specs=pl.BlockSpec(memory_space=pltpu.VMEM),
        scratch_shapes=[
            pltpu.VMEM(queries.shape, queries.dtype),
            pltpu.VMEM((passage_count // 128, 128), passage_len.dtype),
            pltpu.VMEM((1, query_count), query_len.dtype),
            pltpu.VMEM(passages.shape, passages.dtype),
            pltpu.VMEM((2 * per_chunk * token_count, width), jnp.bfloat16),
            pltpu.VMEM((row_count, width), jnp.float32),
            pltpu.VMEM((width, row_count), jnp.bfloat16),
            pltpu.VMEM((passage_count, 128), jnp.float32),
            maxima,
            maxima,
            maxima,
            maxima,
            pltpu.VMEM((ny, chunks, per_chunk, query_count), jnp.float32),
            pltpu.VMEM((max(1, half_blocks - 1), block_rows, query_count), jnp.float32),
            pltpu.VMEM((block_rows, query_count), jnp.float32),
            pltpu.VMEM((nx + nz, 8, query_count), jnp.float32),
            dma((3,)),
            dma((2 * chunks,)),
            dma((2,)),
            dma((chunks, PARTS)),
            dma((chunks, PARTS)),
            dma((ny,)),
            dma((ny, half_blocks)),
            dma((max(1, half_blocks - 1),)),
            dma,
            dma((nx + nz,)),
            dma((nx + nz,)),
        ],
        compiler_params=pltpu.CompilerParams(
            collective_id=0, has_side_effects=True, vmem_limit_bytes=67043328
        ),
    )(
        queries,
        passage_len.reshape(passage_count // 128, 128),
        query_len.reshape(1, query_count),
        passages,
    )


def solution(mesh):
    sizes = tuple(mesh.shape[name] for name in ("gx", "gy", "gz"))
    return jax.shard_map(
        functools.partial(shards, sizes),
        mesh=mesh,
        in_specs=(P(None, "gy", None), P("gx", "gz", None), P("gx"), P()),
        out_specs=P(None, ("gx", "gz")),
        check_vma=False,
    )
```

profile of v0, /device:TPU:0, one launch (start us, length us, event | category | flops | bytes accessed | tf_op | source)
XLA Modules:
  0.0 48.6 jit_solution(777773839192928643)
XLA Ops:
  0.0 47.2 %shard_map.46 = f32[128,128]{1,0:T(8,128)} custom-call(bf16[128,8,128]{2,1,0:T(8,128)(2,1)} %queries_in.1, s32[4,128]{1,0:T(4,128)} %bitcast.2, s32[1,128]{1,0:T(1,128)} %bitcast.3, bf16[512,64,128]{2,1,0:T(8,128)(2,1)} %passages.1), custom_call_target="tpu_custom_call" | custom-call | tf_op jit(solution)/shard_map/pallas_call | solution.py:344
  47.2 1.5 %copy.6 = f32[128,128]{1,0:T(8,128)} copy(f32[128,128]{1,0:T(8,128)} %shard_map.46) | data formatting | bytes 131072
where the time goes:
time: 48.8 us; the launch traced here: 48.6 us
  Pallas kernels  47.2 us (97%)
  local copies, waits for them, and re-layouts  1.47 us (3%)
    pallas_call x1, Pallas kernels, shards(): pl.pallas_call(functools.partial(kernel, sizes), out_shape=jax.ShapeDtype...  47.2 us
    unnamed x1, local copies, waits for them, and re-layouts  1.47 us

commit v1 on v0

v1 whole, which is shorter than its diff:
```python
import functools

import jax
import jax.numpy as jnp
from jax import lax
from jax.experimental import pallas as pl
from jax.experimental.pallas import tpu as pltpu
from jax.sharding import PartitionSpec as P

masked_low = -1e30
MESH = pl.DeviceIdType.MESH
UP_LAGS = (3, 3)
DOWN_LAGS = (4, 3)
PEER_LAG = 3
TAIL = 2
PER_CHUNK = 16


def kernel(
    sizes,
    queries_in,
    lengths_in,
    query_len_in,
    passages,
    out,
    queries,
    lengths,
    query_len,
    x,
    masked_x,
    wide_queries,
    query_columns,
    limits,
    own_low,
    own_high,
    got_low,
    got_high,
    partials,
    forward,
    total,
    stats,
    far_tail,
    out_tile,
    small_sem,
    load_sem,
    z_send,
    out_sem,
    low_recv,
    high_recv,
    peer_send,
    peer_recv,
    forward_send,
    forward_recv,
    stat_send,
    stat_recv,
    far_send,
    far_recv,
):
    nx, ny, nz = sizes
    gx, gy, gz = (lax.axis_index(name) for name in ("gx", "gy", "gz"))
    passage_count, token_count, width = x.shape
    query_count, query_rows, _ = queries.shape
    slots, per_chunk, row_count = own_low.shape
    chunks = slots - 1
    half_blocks = nz // 2
    per_block = chunks // half_blocks
    block_rows = passage_count // nz

    def low_start(c):
        return (half_blocks - 1 - c // per_block) * block_rows + (c % per_block) * per_chunk

    def high_start(c):
        return half_blocks * block_rows + c * per_chunk

    barrier = pltpu.get_barrier_semaphore()
    for axis, place, count in (("gx", gx, nx), ("gy", gy, ny)):
        for turn in range(1, count):
            pl.semaphore_signal(
                barrier,
                inc=1,
                device_id={axis: lax.rem(place + turn, count)},
                device_id_type=MESH,
            )
    for has_neighbour, neighbour in ((gz > 0, gz - 1), (gz < nz - 1, gz + 1)):
        @pl.when(has_neighbour)
        def _():
            pl.semaphore_signal(
                barrier, inc=1, device_id={"gz": neighbour}, device_id_type=MESH
            )

    at_end = (gz == 0) | (gz == nz - 1)

    small = [
        pltpu.make_async_copy(source, target, small_sem.at[index])
        for index, (source, target) in enumerate(
            ((queries_in, queries), (lengths_in, lengths), (query_len_in, query_len))
        )
    ]
    for copy in small:
        copy.start()

    def load(start, index):
        rows = pl.ds(start, per_chunk)
        return pltpu.make_async_copy(passages.at[rows], x.at[rows], load_sem.at[index])

    def start_loads(c, carry):
        load(low_start(c), c).start()
        load(high_start(c), chunks + c).start()
        return carry

    lax.fori_loop(0, chunks, start_loads, 0)

    for copy in small:
        copy.wait()

    wide_queries[...] = queries[...].astype(jnp.float32).reshape(row_count, width)
    for i in range(query_rows):
        tile = wide_queries[pl.ds(i, query_count, stride=query_rows), :]
        query_columns[:, i * query_count : (i + 1) * query_count] = tile.T.astype(jnp.bfloat16)

    first_token = (gz * token_count).astype(jnp.float32)
    for b in range(passage_count // 128):
        row = lengths[b : b + 1, :].astype(jnp.float32) - first_token
        limits[b * 128 : (b + 1) * 128, :] = jnp.broadcast_to(row, (128, 128)).T

    token_ids = lax.broadcasted_iota(jnp.int32, (token_count, width), 0).astype(jnp.float32)
    tile_columns = 256

    def compute(c):
        starts = (low_start(c), high_start(c))
        limit = []
        for half, start in enumerate(starts):
            for p in range(per_chunk):
                tokens = x[start + p].astype(jnp.float32)
                usable = token_ids < limits[pl.ds(start + p, 1), :]
                tokens = jnp.where(usable, tokens, tokens[0:1, :])
                row = (half * per_chunk + p) * token_count
                masked_x[row : row + token_count, :] = tokens.astype(jnp.bfloat16)
            limit.append(limits[pl.ds(start, per_chunk), :])
        limit = jnp.concatenate(limit, axis=0)
        any_used = jnp.concatenate([limit] * (tile_columns // 128), axis=1) > 0.0
        for t in range(row_count // tile_columns):
            columns = slice(t * tile_columns, (t + 1) * tile_columns)
            scores = jnp.dot(
                masked_x[...], query_columns[:, columns], preferred_element_type=jnp.float32
            )
            best = jnp.max(scores.reshape(2 * per_chunk, token_count, tile_columns), axis=1)
            best = jnp.where(any_used, best, masked_low)
            own_low[c, :, columns] = best[:per_chunk]
            own_high[c, :, columns] = best[per_chunk:]

    class Flow:
        def __init__(self, own, got, recv, index, hops, lags, target):
            self.own, self.got, self.recv, self.index = own, got, recv, index
            self.target = target
            self.is_first, self.is_last = hops == 0, hops == nz - 1
            self.is_inner = (hops > 0) & (hops < nz - 1)
            self.lag = lags[0] + lags[1] * (hops - 1)

        def copy(self, source, c):
            return pltpu.make_async_remote_copy(
                src_ref=source.at[c],
                dst_ref=self.got.at[c],
                send_sem=z_send.at[self.index],
                recv_sem=self.recv.at[c],
                device_id={"gz": self.target},
                device_id_type=MESH,
            )

        def merge(self, c):
            self.got[c] = jnp.maximum(self.got[c], self.own[c])

    first, last = gz == 0, gz == nz - 1
    below, above = lax.rem(gz + nz - 1, nz), lax.rem(gz + 1, nz)
    low = Flow(own_low, got_low, low_recv, 0, nz - 1 - gz, DOWN_LAGS, below)
    high = Flow(own_high, got_high, high_recv, 1, gz, UP_LAGS, above)
    flows = (low, high)

    def peer_copy(turn, slot, block, where):
        return pltpu.make_async_remote_copy(
            src_ref=partials.at[(slot, *where)],
            dst_ref=partials.at[(slot, *where)],
            send_sem=peer_send.at[turn],
            recv_sem=peer_recv.at[slot, block],
            device_id={"gy": lax.rem(gy + turn, ny)},
            device_id_type=MESH,
        )

    def finalise(merged, c):
        counted = query_len[...] - gy * query_rows
        so_far = jnp.zeros((per_chunk, query_count), jnp.float32)
        for i in range(query_rows):
            values = merged[c, :, i * query_count : (i + 1) * query_count]
            so_far = so_far + jnp.where(counted > i, values, 0.0)
        partials[gy, c] = so_far
        for turn in range(1, ny):
            peer_copy(turn, gy, piece_of(c), (c,)).start()

    def piece_of(c):
        return c // per_block + jnp.where(c >= chunks - TAIL, 1, 0)

    def piece_total(piece):
        start = piece * per_block if piece < half_blocks else chunks - TAIL
        count = TAIL if piece == half_blocks else per_block - TAIL * (piece == half_blocks - 1)
        where = pl.ds(start, count)
        for turn in range(1, ny):
            slot = lax.rem(gy + turn, ny)
            peer_copy(turn, slot, piece, (where,)).wait_recv()
        summed = partials[0, where]
        for slot in range(1, ny):
            summed = summed + partials[slot, where]
        return summed.reshape(count * per_chunk, query_count)

    def far_copy(turn, slot):
        tail = pl.ds(chunks - TAIL, TAIL)
        return pltpu.make_async_remote_copy(
            src_ref=partials.at[slot, tail],
            dst_ref=far_tail.at[slot],
            send_sem=far_send.at[turn],
            recv_sem=far_recv.at[slot],
            device_id={"gy": lax.rem(gy + turn, ny), "gz": 0},
            device_id_type=MESH,
        )

    def forward_copy(block):
        target = jnp.where(gz == 0, half_blocks - 1 - block, half_blocks + block)
        return pltpu.make_async_remote_copy(
            src_ref=forward.at[block],
            dst_ref=total,
            send_sem=forward_send.at[block],
            recv_sem=forward_recv,
            device_id={"gz": target},
            device_id_type=MESH,
        )

    def receive(flow, c):
        flow.copy(flow.got, c).wait_recv()
        flow.merge(c)
        flow.copy(flow.got, c).start()

    def ready(s):
        load(low_start(s), s).wait()
        load(high_start(s), chunks + s).wait()
        compute(s)

    def send(flow, c):
        @pl.when(flow.is_first)
        def _():
            flow.copy(flow.own, c).start()

    def pass_on(s):
        for flow in flows:
            c = s - flow.lag

            @pl.when(flow.is_inner & (c >= 0) & (c < chunks))
            def _():
                receive(flow, c)

    def head(s, carry):
        ready(s)
        return carry

    def head_send(c, carry):
        for flow in flows:
            send(flow, c)
        return carry

    def step(s, carry):
        pass_on(s)
        ready(s)
        for flow in flows:
            send(flow, s)
        return carry

    def drain(s, carry):
        pass_on(s)
        return carry

    last_lag = max(lags[0] + lags[1] * (nz - 3) for lags in (UP_LAGS, DOWN_LAGS))
    head_steps = 1
    lax.fori_loop(0, head_steps, head, 0)
    pl.semaphore_wait(barrier, nx + ny - 2 + jnp.where(at_end, 1, 2))
    lax.fori_loop(0, head_steps, head_send, 0)
    lax.fori_loop(head_steps, chunks, step, 0)

    @pl.when(jnp.logical_not(at_end))
    def _():
        lax.fori_loop(chunks, chunks + last_lag, drain, 0)

    for flow in flows:
        @pl.when(flow.is_last)
        def _():
            def collect(c, carry):
                flow.copy(flow.got, c).wait_recv()
                flow.merge(c)
                finalise(flow.got, c)
                for block in range(half_blocks - 1):
                    @pl.when(c == (block + 1) * per_block - 1 + PEER_LAG)
                    def _():
                        forward[block] = piece_total(block)
                        forward_copy(block).start()
                return carry

            lax.fori_loop(0, chunks, collect, 0)

    main_rows = block_rows - TAIL * per_chunk
    row_ids = lax.broadcasted_iota(jnp.int32, stats.shape[1:], 0)

    def stat_copy(axis, base, place, count, slot, turn):
        return pltpu.make_async_remote_copy(
            src_ref=stats.at[base + slot],
            dst_ref=stats.at[base + slot],
            send_sem=stat_send.at[base + turn],
            recv_sem=stat_recv.at[base + slot],
            device_id={axis: lax.rem(place + turn, count)},
            device_id_type=MESH,
        )

    def share(axis, base, place, count, slot):
        for turn in range(1, count):
            stat_copy(axis, base, place, count, slot, turn).start()

    def pair(top, summed):
        return jnp.where(row_ids == 0, top, summed)

    def joined(pairs):
        highest = functools.reduce(jnp.maximum, [top for top, _ in pairs])
        shares = [summed * jnp.exp(top - highest) for top, summed in pairs]
        return highest, functools.reduce(jnp.add, shares)

    def summary(blocks):
        tops = [jnp.max(block, axis=0, keepdims=True) for block in blocks]
        top = functools.reduce(jnp.maximum, tops)
        sums = [jnp.sum(jnp.exp(block - top), axis=0, keepdims=True) for block in blocks]
        return top, functools.reduce(jnp.add, sums)

    def read(slot):
        return stats[slot, 0:1, :], stats[slot, 1:2, :]

    def main_summary():
        total[pl.ds(0, main_rows), :] = piece_total(half_blocks - 1)
        blocks = [forward[block] for block in range(half_blocks - 1)]
        return summary(blocks + [total[pl.ds(0, main_rows), :]])

    far_stat = stat_copy("gz", nx, gz, nz, 0, 1)
    final_stat = stat_copy("gz", nx, gz, nz, 1, 1)

    @pl.when(last)
    def _():
        for turn in range(ny):
            far_copy(turn, gy).start()
        stats[nx] = pair(*main_summary())
        far_stat.start()
        total[pl.ds(main_rows, TAIL * per_chunk), :] = piece_total(half_blocks)

    @pl.when(jnp.logical_not(at_end))
    def _():
        forward_copy(0).wait_recv()

    @pl.when(first)
    def _():
        main = main_summary()
        total[pl.ds(main_rows, TAIL * per_chunk), :] = piece_total(half_blocks)
        for slot in range(ny):
            far_copy(0, slot).wait_recv()
        far = functools.reduce(jnp.add, [far_tail[slot] for slot in range(ny)])
        blocks = [total[pl.ds(main_rows, TAIL * per_chunk), :], far.reshape(-1, query_count)]
        far_stat.wait_recv()
        stats[gx] = pair(*joined([main, summary(blocks), read(nx)]))
        share("gx", 0, gx, nx, gx)
        for turn in range(1, nx):
            stat_copy("gx", 0, gx, nx, lax.rem(gx + turn, nx), turn).wait_recv()
        stats[nx + 1] = pair(*joined([read(slot) for slot in range(nx)]))
        share("gz", nx, gz, nz, 1)

    @pl.when(jnp.logical_not(first))
    def _():
        final_stat.wait_recv()

    top, summed = read(nx + 1)
    scores = total[...]
    out_tile[...] = (scores - (top + jnp.log(summed))).T
    result = pltpu.make_async_copy(out_tile, out, out_sem)
    result.start()

    for flow in flows:
        @pl.when(jnp.logical_not(flow.is_last))
        def _():
            whole = pl.ds(0, chunks)
            pltpu.make_async_remote_copy(
                src_ref=flow.got.at[whole],
                dst_ref=flow.got.at[whole],
                send_sem=z_send.at[flow.index],
                recv_sem=flow.recv.at[0],
                device_id={"gz": flow.target},
                device_id_type=MESH,
            ).wait_send()

    @pl.when(at_end)
    def _():
        for turn in range(1, ny):
            peer_copy(turn, gy, 0, (pl.ds(0, chunks),)).wait_send()
        for block in range(half_blocks - 1):
            forward_copy(block).wait_send()

    @pl.when(last)
    def _():
        for turn in range(ny):
            far_copy(turn, gy).wait_send()
        far_stat.wait_send()

    @pl.when(first)
    def _():
        for axis, base, place, count, slot in (("gx", 0, gx, nx, gx), ("gz", nx, gz, nz, 1)):
            for turn in range(1, count):
                stat_copy(axis, base, place, count, slot, turn).wait_send()

    result.wait()


def shards(sizes, queries, passages, passage_len, query_len):
    nx, ny, nz = sizes
    query_count, query_rows, width = queries.shape
    passage_count, token_count, _ = passages.shape
    row_count = query_count * query_rows
    block_rows = passage_count // nz
    per_chunk = PER_CHUNK
    chunks = passage_count // 2 // per_chunk
    half_blocks = nz // 2
    maxima = pltpu.VMEM((chunks + 1, per_chunk, row_count), jnp.float32)
    dma = pltpu.SemaphoreType.DMA
    anywhere = pl.BlockSpec(memory_space=pltpu.HBM)
    return pl.pallas_call(
        functools.partial(kernel, sizes),
        out_shape=jax.ShapeDtypeStruct((query_count, block_rows), jnp.float32),
        in_specs=[anywhere] * 4,
        out_specs=anywhere,
        scratch_shapes=[
            pltpu.VMEM(queries.shape, queries.dtype),
            pltpu.VMEM((passage_count // 128, 128), passage_len.dtype),
            pltpu.VMEM((1, query_count), query_len.dtype),
            pltpu.VMEM(passages.shape, passages.dtype),
            pltpu.VMEM((2 * per_chunk * token_count, width), jnp.bfloat16),
            pltpu.VMEM((row_count, width), jnp.float32),
            pltpu.VMEM((width, row_count), jnp.bfloat16),
            pltpu.VMEM((passage_count, 128), jnp.float32),
            maxima,
            maxima,
            maxima,
            maxima,
            pltpu.VMEM((ny, chunks, per_chunk, query_count), jnp.float32),
            pltpu.VMEM((max(1, half_blocks - 1), block_rows, query_count), jnp.float32),
            pltpu.VMEM((block_rows, query_count), jnp.float32),
            pltpu.VMEM((nx + 2, 8, query_count), jnp.float32),
            pltpu.VMEM((ny, TAIL, per_chunk, query_count), jnp.float32),
            pltpu.VMEM((query_count, block_rows), jnp.float32),
            dma((3,)),
            dma((2 * chunks,)),
            dma((2,)),
            dma,
            dma((chunks,)),
            dma((chunks,)),
            dma((ny,)),
            dma((ny, half_blocks + 1)),
            dma((max(1, half_blocks - 1),)),
            dma,
            dma((nx + nz,)),
            dma((nx + nz,)),
            dma((ny,)),
            dma((ny,)),
        ],
        compiler_params=pltpu.CompilerParams(
            collective_id=0, has_side_effects=True, vmem_limit_bytes=67043328
        ),
    )(
        queries,
        passage_len.reshape(passage_count // 128, 128),
        query_len.reshape(1, query_count),
        passages,
    )


def solution(mesh):
    sizes = tuple(mesh.shape[name] for name in ("gx", "gy", "gz"))
    return jax.shard_map(
        functools.partial(shards, sizes),
        mesh=mesh,
        in_specs=(P(None, "gy", None), P("gx", "gz", None), P("gx"), P()),
        out_specs=P(None, ("gx", "gz")),
        check_vma=False,
    )
```

time: 48.8 us -> 46.5 us (0.953)
  Pallas kernels: 47.2 us -> 44.5 us
    pallas_call x1, Pallas kernels: 47.2 us -> 44.5 us  [shards(): pl.pallas_call(functools.partial(kernel, sizes), out_shape=jax.ShapeDtype...]
where the time goes in v1:
time: 46.5 us; the launch traced here: 46 us
  Pallas kernels  44.5 us (96%)
  local copies, waits for them, and re-layouts  1.47 us (3%)
    pallas_call x1, Pallas kernels, shards(): pl.pallas_call(functools.partial(kernel, sizes), out_shape=jax.ShapeDtype...  44.5 us
    unnamed x1, local copies, waits for them, and re-layouts  1.47 us

profile of v1, /device:TPU:0, one launch (start us, length us, event | category | flops | bytes accessed | tf_op | source)
XLA Modules:
  0.0 46.0 jit_solution(11782195905483137744)
XLA Ops:
  0.0 44.5 %shard_map.46 = f32[128,128]{1,0:T(8,128)} custom-call(bf16[128,8,128]{2,1,0:T(8,128)(2,1)} %queries_in.1, s32[4,128]{1,0:T(4,128)} %bitcast.2, s32[1,128]{1,0:T(1,128)} %bitcast.3, bf16[512,64,128]{2,1,0:T(8,128)(2,1)} %passages.1), custom_call_target="tpu_custom_call" | custom-call | tf_op jit(solution)/shard_map/pallas_call | solution.py:433
  44.5 1.5 %copy.6 = f32[128,128]{1,0:T(8,128)} copy(f32[128,128]{1,0:T(8,128)} %shard_map.46) | data formatting | bytes 131072

commit v2 on v1

v2 whole, which is shorter than its diff:
```python
import functools

import jax
import jax.numpy as jnp
from jax import lax
from jax.experimental import pallas as pl
from jax.experimental.pallas import tpu as pltpu
from jax.sharding import PartitionSpec as P

masked_low = -1e30
MESH = pl.DeviceIdType.MESH
UP_LAGS = ((3, 3), (2, 2), (3, 3), (2, 2))
DOWN_LAGS = ((4, 3), (3, 2), (4, 3), (3, 2))
TAIL_PARTS = 2
PEER_LAG = 3
TAIL = 2
VMEM_BYTES = 67043328
PER_CHUNK = 16


def kernel(
    sizes,
    queries_in,
    lengths_in,
    query_len_in,
    passages,
    out,
    queries,
    lengths,
    query_len,
    x,
    masked_x,
    wide_queries,
    query_columns,
    limits,
    own,
    got,
    partials,
    forward,
    total,
    stats,
    far_tail,
    small_sem,
    load_sem,
    z_send,
    z_recv,
    peer_send,
    peer_recv,
    forward_send,
    forward_recv,
    stat_send,
    stat_recv,
    far_send,
    far_recv,
):
    nx, ny, nz = sizes
    gx, gy, gz = (lax.axis_index(name) for name in ("gx", "gy", "gz"))
    passage_count, token_count, width = x.shape
    query_count, query_rows, _ = queries.shape
    _, chunks, per_chunk, row_count = own.shape
    tail_rows = per_chunk // TAIL_PARTS
    half_blocks = nz // 2
    per_block = chunks // half_blocks
    block_rows = passage_count // nz

    def low_start(c):
        return (half_blocks - 1 - c // per_block) * block_rows + (c % per_block) * per_chunk

    def high_start(c):
        return half_blocks * block_rows + c * per_chunk

    small = [
        pltpu.make_async_copy(source, target, small_sem.at[index])
        for index, (source, target) in enumerate(
            ((queries_in, queries), (lengths_in, lengths), (query_len_in, query_len))
        )
    ]
    for copy in small:
        copy.start()

    barrier = pltpu.get_barrier_semaphore()
    for axis, place, count in (("gx", gx, nx), ("gy", gy, ny)):
        for turn in range(1, count):
            pl.semaphore_signal(
                barrier,
                inc=1,
                device_id={axis: lax.rem(place + turn, count)},
                device_id_type=MESH,
            )
    for has_neighbour, neighbour in ((gz > 0, gz - 1), (gz < nz - 1, gz + 1)):
        @pl.when(has_neighbour)
        def _():
            pl.semaphore_signal(
                barrier, inc=1, device_id={"gz": neighbour}, device_id_type=MESH
            )

    at_end = (gz == 0) | (gz == nz - 1)

    def load(start, rows, group):
        rows = pl.ds(start, rows)
        return pltpu.make_async_copy(passages.at[rows], x.at[rows], load_sem.at[group])

    group_rows = (per_chunk, block_rows - per_chunk) + (block_rows,) * (half_blocks - 1)
    for group, rows in enumerate(group_rows):
        c = group if group < 2 else (group - 1) * per_block
        load(low_start(c), rows, group).start()
        load(high_start(c), rows, group).start()

    def wait_load(group):
        load(0, 2 * group_rows[group], group).wait()

    for copy in small:
        copy.wait()

    wide_queries[...] = queries[...].astype(jnp.float32).reshape(row_count, width)
    for i in range(query_rows):
        tile = wide_queries[pl.ds(i, query_count, stride=query_rows), :]
        query_columns[:, i * query_count : (i + 1) * query_count] = tile.T.astype(jnp.bfloat16)

    first_token = (gz * token_count).astype(jnp.float32)
    for b in range(passage_count // 128):
        row = lengths[b : b + 1, :].astype(jnp.float32) - first_token
        limits[b * 128 : (b + 1) * 128, :] = jnp.broadcast_to(row, (128, 128)).T

    token_ids = lax.broadcasted_iota(jnp.int32, (token_count, width), 0).astype(jnp.float32)
    tile_columns = 256

    def compute(c, sides):
        rows = len(sides) * per_chunk
        limit = []
        for place, side in enumerate(sides):
            start = jnp.where(side == 0, low_start(c), high_start(c))
            for p in range(per_chunk):
                tokens = x[start + p].astype(jnp.float32)
                usable = token_ids < limits[pl.ds(start + p, 1), :]
                tokens = jnp.where(usable, tokens, tokens[0:1, :])
                row = (place * per_chunk + p) * token_count
                masked_x[row : row + token_count, :] = tokens.astype(jnp.bfloat16)
            limit.append(limits[pl.ds(start, per_chunk), :])
        limit = jnp.concatenate(limit, axis=0)
        any_used = jnp.concatenate([limit] * (tile_columns // 128), axis=1) > 0.0
        for t in range(row_count // tile_columns):
            columns = slice(t * tile_columns, (t + 1) * tile_columns)
            scores = jnp.dot(
                masked_x[0 : rows * token_count, :],
                query_columns[:, columns],
                preferred_element_type=jnp.float32,
            )
            best = jnp.max(scores.reshape(rows, token_count, tile_columns), axis=1)
            best = jnp.where(any_used, best, masked_low)
            for place, side in enumerate(sides):
                own[side, c, :, columns] = best[place * per_chunk : (place + 1) * per_chunk]

    class Flow:
        def __init__(self, side, hops, lags, target):
            self.side, self.target = side, target
            self.is_first, self.is_last = hops == 0, hops == nz - 1
            self.is_inner = (hops > 0) & (hops < nz - 1)
            even, odd, late_even, late_odd = (start + more * (hops - 1) for start, more in lags)
            self.lag = jnp.where(
                lax.rem(gx, 2) == 0,
                jnp.where(gy == 0, even, late_even),
                jnp.where(gy == 0, odd, late_odd),
            )

        def copy(self, source, where, index):
            return pltpu.make_async_remote_copy(
                src_ref=source.at[(self.side, *where)],
                dst_ref=got.at[(self.side, *where)],
                send_sem=z_send.at[self.side],
                recv_sem=z_recv.at[self.side, index],
                device_id={"gz": self.target},
                device_id_type=MESH,
            )

        def merge(self, where):
            where = (self.side, *where)
            got[where] = jnp.maximum(got[where], own[where])

    def pieces(c, act):
        @pl.when(c < chunks - 1)
        def _():
            act((c,), c)

        @pl.when(c == chunks - 1)
        def _():
            for part in range(TAIL_PARTS):
                act((c, pl.ds(part * tail_rows, tail_rows)), c + part)

    first, last = gz == 0, gz == nz - 1
    below, above = lax.rem(gz + nz - 1, nz), lax.rem(gz + 1, nz)
    low = Flow(0, nz - 1 - gz, DOWN_LAGS, below)
    high = Flow(1, gz, UP_LAGS, above)
    flows = (low, high)

    def peer_copy(turn, slot, block, where):
        return pltpu.make_async_remote_copy(
            src_ref=partials.at[(slot, *where)],
            dst_ref=partials.at[(slot, *where)],
            send_sem=peer_send,
            recv_sem=peer_recv.at[slot, block],
            device_id={"gy": lax.rem(gy + turn, ny)},
            device_id_type=MESH,
        )

    def finalise(side, c):
        counted = query_len[...] - gy * query_rows
        so_far = jnp.zeros((per_chunk, query_count), jnp.float32)
        for i in range(query_rows):
            values = got[side, c, :, i * query_count : (i + 1) * query_count]
            so_far = so_far + jnp.where(counted > i, values, 0.0)
        partials[gy, c] = so_far

        @pl.when(last & (c >= chunks - TAIL))
        def _():
            for turn in reversed(range(ny)):
                far_copy(turn, gy, c - (chunks - TAIL)).start()

        for turn in range(1, ny):
            peer_copy(turn, gy, piece_of(c), (c,)).start()

    def piece_of(c):
        return c // per_block + jnp.where(c >= chunks - TAIL, 1, 0)

    def piece_total(piece):
        start = piece * per_block if piece < half_blocks else chunks - TAIL
        count = TAIL if piece == half_blocks else per_block - TAIL * (piece == half_blocks - 1)
        where = pl.ds(start, count)
        for turn in range(1, ny):
            slot = lax.rem(gy + turn, ny)
            peer_copy(turn, slot, piece, (where,)).wait_recv()
        summed = partials[0, where]
        for slot in range(1, ny):
            summed = summed + partials[slot, where]
        return summed.reshape(count * per_chunk, query_count)

    def far_copy(turn, slot, piece):
        return pltpu.make_async_remote_copy(
            src_ref=partials.at[slot, chunks - TAIL + piece],
            dst_ref=far_tail.at[slot, piece],
            send_sem=far_send,
            recv_sem=far_recv.at[slot, piece],
            device_id={"gy": lax.rem(gy + turn, ny), "gz": 0},
            device_id_type=MESH,
        )

    def forward_copy(block):
        target = jnp.where(gz == 0, half_blocks - 1 - block, half_blocks + block)
        return pltpu.make_async_remote_copy(
            src_ref=forward.at[block],
            dst_ref=total,
            send_sem=forward_send.at[block],
            recv_sem=forward_recv,
            device_id={"gz": target},
            device_id_type=MESH,
        )

    def pass_on(s):
        for flow in flows:
            c = s - flow.lag

            @pl.when(flow.is_inner & (c >= 0) & (c < chunks))
            def _():
                def act(where, index):
                    flow.copy(got, where, index).wait_recv()
                    flow.merge(where)
                    flow.copy(got, where, index).start()

                pieces(c, act)

    def send(c):
        for flow in flows:
            @pl.when(flow.is_first)
            def _():
                pieces(c, lambda where, index: flow.copy(own, where, index).start())

    def step(s, carry):
        pass_on(s)
        for group in range(1, len(group_rows)):
            @pl.when(s == (1 if group == 1 else (group - 1) * per_block))
            def _():
                wait_load(group)

        compute(s, (0, 1))
        send(s)
        return carry

    def drain(s, carry):
        pass_on(s)
        return carry

    urgent = jnp.where(gz < half_blocks, 1, 0)
    wait_load(0)
    compute(0, (urgent,))
    pl.semaphore_wait(barrier, nx + ny - 2 + jnp.where(at_end, 1, 2))
    send(0)
    compute(0, (1 - urgent,))
    lax.fori_loop(1, chunks, step, 0)

    @pl.when(jnp.logical_not(at_end))
    def _():
        last_lag = max(start + more * (nz - 3) for start, more in UP_LAGS + DOWN_LAGS)
        lax.fori_loop(chunks, chunks + last_lag, drain, 0)

    for flow in flows:
        @pl.when(flow.is_last)
        def _():
            def collect(c, carry):
                def act(where, index):
                    flow.copy(got, where, index).wait_recv()
                    flow.merge(where)

                pieces(c, act)
                finalise(flow.side, c)
                for block in range(half_blocks - 1):
                    @pl.when(c == (block + 1) * per_block - 1 + PEER_LAG)
                    def _():
                        forward[block] = piece_total(block)
                        forward_copy(block).start()
                return carry

            lax.fori_loop(0, chunks, collect, 0)

    main_rows = block_rows - TAIL * per_chunk
    row_ids = lax.broadcasted_iota(jnp.int32, stats.shape[1:], 0)

    def stat_copy(slot, to_x, to_z):
        return pltpu.make_async_remote_copy(
            src_ref=stats.at[slot],
            dst_ref=stats.at[slot],
            send_sem=stat_send,
            recv_sem=stat_recv.at[slot],
            device_id={"gx": to_x, "gz": to_z},
            device_id_type=MESH,
        )

    def pair(top, summed):
        return jnp.where(row_ids == 0, top, summed)

    def joined(pairs):
        highest = functools.reduce(jnp.maximum, [top for top, _ in pairs])
        shares = [summed * jnp.exp(top - highest) for top, summed in pairs]
        return highest, functools.reduce(jnp.add, shares)

    def summary(blocks):
        tops = [jnp.max(block, axis=0, keepdims=True) for block in blocks]
        top = functools.reduce(jnp.maximum, tops)
        sums = [jnp.sum(jnp.exp(block - top), axis=0, keepdims=True) for block in blocks]
        return top, functools.reduce(jnp.add, sums)

    def read(slot):
        return stats[slot, 0:1, :], stats[slot, 1:2, :]

    def main_summary():
        total[pl.ds(0, main_rows), :] = piece_total(half_blocks - 1)
        blocks = [forward[block] for block in range(half_blocks - 1)]
        return summary(blocks + [total[pl.ds(0, main_rows), :]])

    far_stat = stat_copy(nx, gx, 0)

    @pl.when(last)
    def _():
        stats[nx] = pair(*main_summary())
        far_stat.start()
        total[pl.ds(main_rows, TAIL * per_chunk), :] = piece_total(half_blocks)

    @pl.when(jnp.logical_not(at_end))
    def _():
        forward_copy(0).wait_recv()

    @pl.when(first)
    def _():
        main = main_summary()
        total[pl.ds(main_rows, TAIL * per_chunk), :] = piece_total(half_blocks)
        for slot in range(ny):
            for piece in range(TAIL):
                far_copy(0, slot, piece).wait_recv()
        far = functools.reduce(jnp.add, [far_tail[slot] for slot in range(ny)])
        blocks = [total[pl.ds(main_rows, TAIL * per_chunk), :], far.reshape(-1, query_count)]
        far_stat.wait_recv()
        stats[gx] = pair(*joined([main, summary(blocks), read(nx)]))
        for turn in range(1, nx * nz):
            stat_copy(gx, lax.rem(gx + turn % nx, nx), turn // nx).start()
        for turn in range(1, nx):
            stat_copy(lax.rem(gx + turn, nx), gx, gz).wait_recv()

    @pl.when(jnp.logical_not(first))
    def _():
        for slot in range(nx):
            stat_copy(slot, gx, gz).wait_recv()

    top, summed = joined([read(slot) for slot in range(nx)])
    scores = total[...]
    out[...] = (scores - (top + jnp.log(summed))).T

    def wait_sent(whole, sem):
        pltpu.make_async_remote_copy(
            src_ref=whole,
            dst_ref=whole,
            send_sem=sem,
            recv_sem=forward_recv,
            device_id={"gz": below},
            device_id_type=MESH,
        ).wait_send()

    for flow in flows:
        @pl.when(jnp.logical_not(flow.is_last))
        def _():
            wait_sent(got.at[flow.side], z_send.at[flow.side])

    @pl.when(at_end)
    def _():
        wait_sent(partials.at[pl.ds(0, ny - 1)], peer_send)
        for block in range(half_blocks - 1):
            forward_copy(block).wait_send()

    @pl.when(last)
    def _():
        wait_sent(far_tail, far_send)
        far_stat.wait_send()

    @pl.when(first)
    def _():
        wait_sent(stats.at[pl.ds(0, nx * nz - 1)], stat_send)


def shards(sizes, queries, passages, passage_len, query_len):
    nx, ny, nz = sizes
    query_count, query_rows, width = queries.shape
    passage_count, token_count, _ = passages.shape
    row_count = query_count * query_rows
    block_rows = passage_count // nz
    per_chunk = PER_CHUNK
    chunks = passage_count // 2 // per_chunk
    half_blocks = nz // 2
    maxima = pltpu.VMEM((2, chunks, per_chunk, row_count), jnp.float32)
    dma = pltpu.SemaphoreType.DMA
    anywhere = pl.BlockSpec(memory_space=pltpu.HBM)
    return pl.pallas_call(
        functools.partial(kernel, sizes),
        out_shape=pltpu.VMEM((query_count, block_rows), jnp.float32),
        in_specs=[anywhere] * 4,
        out_specs=pl.BlockSpec(memory_space=pltpu.VMEM),
        scratch_shapes=[
            pltpu.VMEM(queries.shape, queries.dtype),
            pltpu.VMEM((passage_count // 128, 128), passage_len.dtype),
            pltpu.VMEM((1, query_count), query_len.dtype),
            pltpu.VMEM(passages.shape, passages.dtype),
            pltpu.VMEM((2 * per_chunk * token_count, width), jnp.bfloat16),
            pltpu.VMEM((row_count, width), jnp.float32),
            pltpu.VMEM((width, row_count), jnp.bfloat16),
            pltpu.VMEM((passage_count, 128), jnp.float32),
            maxima,
            maxima,
            pltpu.VMEM((ny, chunks, per_chunk, query_count), jnp.float32),
            pltpu.VMEM((max(1, half_blocks - 1), block_rows, query_count), jnp.float32),
            pltpu.VMEM((block_rows, query_count), jnp.float32),
            pltpu.VMEM((max(nx + 1, nx * nz - 1), 8, query_count), jnp.float32),
            pltpu.VMEM((ny, TAIL, per_chunk, query_count), jnp.float32),
            dma((3,)),
            dma((half_blocks + 1,)),
            dma((2,)),
            dma((2, chunks + TAIL_PARTS - 1)),
            dma,
            dma((ny, half_blocks + 1)),
            dma((max(1, half_blocks - 1),)),
            dma,
            dma,
            dma((nx + 1,)),
            dma,
            dma((ny, TAIL)),
        ],
        compiler_params=pltpu.CompilerParams(
            collective_id=0, has_side_effects=True, vmem_limit_bytes=VMEM_BYTES - 4 * query_count * block_rows
        ),
    )(
        queries,
        passage_len.reshape(passage_count // 128, 128),
        query_len.reshape(1, query_count),
        passages,
    )


def solution(mesh):
    sizes = tuple(mesh.shape[name] for name in ("gx", "gy", "gz"))
    return jax.shard_map(
        functools.partial(shards, sizes),
        mesh=mesh,
        in_specs=(P(None, "gy", None), P("gx", "gz", None), P("gx"), P()),
        out_specs=P(None, ("gx", "gz")),
        check_vma=False,
    )
```

time: 46.5 us -> 44.6 us (0.959)
  local copies, waits for them, and re-layouts: 1.47 us -> 0.63 us
  Pallas kernels: 44.5 us -> 43.8 us
    unnamed x1, local copies, waits for them, and re-layouts: 1.47 us -> 0.63 us
    pallas_call x1, Pallas kernels: 44.5 us -> 43.8 us  [shards(): pl.pallas_call(functools.partial(kernel, sizes), out_shape=pltpu.VMEM((qu...]
where the time goes in v2:
time: 44.6 us; the launch traced here: 44.4 us
  Pallas kernels  43.8 us (98%)
  local copies, waits for them, and re-layouts  0.63 us (1%)
    pallas_call x1, Pallas kernels, shards(): pl.pallas_call(functools.partial(kernel, sizes), out_shape=pltpu.VMEM((qu...  43.8 us

profile of v2, /device:TPU:0, one launch (start us, length us, event | category | flops | bytes accessed | tf_op | source)
XLA Modules:
  0.0 44.4 jit_solution(3898098101674477670)
XLA Ops:
  0.0 43.8 %shard_map.46 = f32[128,128]{1,0:T(8,128)S(1)} custom-call(bf16[128,8,128]{2,1,0:T(8,128)(2,1)} %queries_in.1, s32[4,128]{1,0:T(4,128)} %bitcast.2, s32[1,128]{1,0:T(1,128)} %bitcast.3, bf16[512,64,128]{2,1,0:T(8,128)(2,1)} %passages.1), custom_call_target="tpu_custom_call" | custom-call | tf_op jit(solution)/shard_map/pallas_call | solution.py:439
  43.8 0.6 %copy.6 = f32[128,128]{1,0:T(8,128)} copy(f32[128,128]{1,0:T(8,128)S(1)} %shard_map.46) | data formatting | bytes 131072

commit v3 on v2

--- a/solution.py
+++ b/solution.py
@@ -9,8 +9,8 @@
 
 masked_low = -1e30
 MESH = pl.DeviceIdType.MESH
-UP_LAGS = ((3, 3), (2, 2), (3, 3), (2, 2))
-DOWN_LAGS = ((4, 3), (3, 2), (4, 3), (3, 2))
+UP_LAGS = ((3, 3), (2, 2))
+DOWN_LAGS = ((4, 3), (3, 2))
 TAIL_PARTS = 2
 PEER_LAG = 3
 TAIL = 2
@@ -109,18 +109,19 @@
     def wait_load(group):
         load(0, 2 * group_rows[group], group).wait()
 
-    for copy in small:
+    for copy in small[1:]:
         copy.wait()
 
+    first_token = (gz * token_count).astype(jnp.float32)
+    for b in range(passage_count // 128):
+        row = lengths[b : b + 1, :].astype(jnp.float32) - first_token
+        limits[b * 128 : (b + 1) * 128, :] = jnp.broadcast_to(row, (128, 128)).T
+
+    small[0].wait()
     wide_queries[...] = queries[...].astype(jnp.float32).reshape(row_count, width)
     for i in range(query_rows):
         tile = wide_queries[pl.ds(i, query_count, stride=query_rows), :]
         query_columns[:, i * query_count : (i + 1) * query_count] = tile.T.astype(jnp.bfloat16)
-
-    first_token = (gz * token_count).astype(jnp.float32)
-    for b in range(passage_count // 128):
-        row = lengths[b : b + 1, :].astype(jnp.float32) - first_token
-        limits[b * 128 : (b + 1) * 128, :] = jnp.broadcast_to(row, (128, 128)).T
 
     token_ids = lax.broadcasted_iota(jnp.int32, (token_count, width), 0).astype(jnp.float32)
     tile_columns = 256
@@ -156,12 +157,8 @@
             self.side, self.target = side, target
             self.is_first, self.is_last = hops == 0, hops == nz - 1
             self.is_inner = (hops > 0) & (hops < nz - 1)
-            even, odd, late_even, late_odd = (start + more * (hops - 1) for start, more in lags)
-            self.lag = jnp.where(
-                lax.rem(gx, 2) == 0,
-                jnp.where(gy == 0, even, late_even),
-                jnp.where(gy == 0, odd, late_odd),
-            )
+            even, odd = (start + more * (hops - 1) for start, more in lags)
+            self.lag = jnp.where(lax.rem(gx, 2) == 0, even, odd)
 
         def copy(self, source, where, index):
             return pltpu.make_async_remote_copy(
@@ -198,7 +195,7 @@
             src_ref=partials.at[(slot, *where)],
             dst_ref=partials.at[(slot, *where)],
             send_sem=peer_send,
-            recv_sem=peer_recv.at[slot, block],
+            recv_sem=peer_recv.at[block],
             device_id={"gy": lax.rem(gy + turn, ny)},
             device_id_type=MESH,
         )
@@ -219,6 +216,16 @@
         for turn in range(1, ny):
             peer_copy(turn, gy, piece_of(c), (c,)).start()
 
+    def wait_landed(whole, sem):
+        pltpu.make_async_remote_copy(
+            src_ref=whole,
+            dst_ref=whole,
+            send_sem=peer_send,
+            recv_sem=sem,
+            device_id={"gz": below},
+            device_id_type=MESH,
+        ).wait_recv()
+
     def piece_of(c):
         return c // per_block + jnp.where(c >= chunks - TAIL, 1, 0)
 
@@ -226,9 +233,7 @@
         start = piece * per_block if piece < half_blocks else chunks - TAIL
         count = TAIL if piece == half_blocks else per_block - TAIL * (piece == half_blocks - 1)
         where = pl.ds(start, count)
-        for turn in range(1, ny):
-            slot = lax.rem(gy + turn, ny)
-            peer_copy(turn, slot, piece, (where,)).wait_recv()
+        wait_landed(partials.at[pl.ds(0, ny - 1), where], peer_recv.at[piece])
         summed = partials[0, where]
         for slot in range(1, ny):
             summed = summed + partials[slot, where]
@@ -239,7 +244,7 @@
             src_ref=partials.at[slot, chunks - TAIL + piece],
             dst_ref=far_tail.at[slot, piece],
             send_sem=far_send,
-            recv_sem=far_recv.at[slot, piece],
+            recv_sem=far_recv,
             device_id={"gy": lax.rem(gy + turn, ny), "gz": 0},
             device_id_type=MESH,
         )
@@ -324,13 +329,13 @@
     main_rows = block_rows - TAIL * per_chunk
     row_ids = lax.broadcasted_iota(jnp.int32, stats.shape[1:], 0)
 
-    def stat_copy(slot, to_x, to_z):
+    def stat_copy(slot, to_x, to_y, to_z, kind=0):
         return pltpu.make_async_remote_copy(
             src_ref=stats.at[slot],
             dst_ref=stats.at[slot],
             send_sem=stat_send,
-            recv_sem=stat_recv.at[slot],
-            device_id={"gx": to_x, "gz": to_z},
+            recv_sem=stat_recv.at[kind],
+            device_id={"gx": to_x, "gy": to_y, "gz": to_z},
             device_id_type=MESH,
         )
 
@@ -356,7 +361,25 @@
         blocks = [forward[block] for block in range(half_blocks - 1)]
         return summary(blocks + [total[pl.ds(0, main_rows), :]])
 
-    far_stat = stat_copy(nx, gx, 0)
+    far_stat = stat_copy(nx, gx, gy, 0, 1)
+    beside = [lax.rem(gx + turn, nx) for turn in range(1, nx)]
+    column = [(lax.rem(gx + turn, nx), to_z) for turn in range(nx) for to_z in range(1, nz)]
+    helper = min(1, ny - 1)
+    shared = (nx - 1, nx - 1 + len(column), nx - 1 + 2 * len(column))
+
+    def shares(act):
+        @pl.when((gy == 0) & (helper != 0))
+        def _():
+            act(0)
+
+        @pl.when((gy != helper) & (gy != 0))
+        def _():
+            act(1)
+
+        @pl.when(gy == helper)
+        def _():
+            act(2 if helper else 1)
+
 
     @pl.when(last)
     def _():
@@ -372,22 +395,25 @@
     def _():
         main = main_summary()
         total[pl.ds(main_rows, TAIL * per_chunk), :] = piece_total(half_blocks)
-        for slot in range(ny):
-            for piece in range(TAIL):
-                far_copy(0, slot, piece).wait_recv()
+        wait_landed(far_tail, far_recv)
         far = functools.reduce(jnp.add, [far_tail[slot] for slot in range(ny)])
         blocks = [total[pl.ds(main_rows, TAIL * per_chunk), :], far.reshape(-1, query_count)]
         far_stat.wait_recv()
         stats[gx] = pair(*joined([main, summary(blocks), read(nx)]))
-        for turn in range(1, nx * nz):
-            stat_copy(gx, lax.rem(gx + turn % nx, nx), turn // nx).start()
-        for turn in range(1, nx):
-            stat_copy(lax.rem(gx + turn, nx), gx, gz).wait_recv()
+        for to_x in beside:
+            stat_copy(gx, to_x, gy, gz).start()
+
+        def share(columns):
+            for to_y in (gy, 0)[:columns]:
+                for to_x, to_z in column:
+                    stat_copy(gx, to_x, to_y, to_z).start()
+
+        shares(share)
+        wait_landed(stats.at[pl.ds(0, nx - 1)], stat_recv.at[0])
 
     @pl.when(jnp.logical_not(first))
     def _():
-        for slot in range(nx):
-            stat_copy(slot, gx, gz).wait_recv()
+        wait_landed(stats.at[pl.ds(0, nx)], stat_recv.at[0])
 
     top, summed = joined([read(slot) for slot in range(nx)])
     scores = total[...]
@@ -421,7 +447,7 @@
 
     @pl.when(first)
     def _():
-        wait_sent(stats.at[pl.ds(0, nx * nz - 1)], stat_send)
+        shares(lambda columns: wait_sent(stats.at[pl.ds(0, shared[columns])], stat_send))
 
 
 def shards(sizes, queries, passages, passage_len, query_len):
@@ -455,20 +481,20 @@
             pltpu.VMEM((ny, chunks, per_chunk, query_count), jnp.float32),
             pltpu.VMEM((max(1, half_blocks - 1), block_rows, query_count), jnp.float32),
             pltpu.VMEM((block_rows, query_count), jnp.float32),
-            pltpu.VMEM((max(nx + 1, nx * nz - 1), 8, query_count), jnp.float32),
+            pltpu.VMEM((nx * (2 * nz - 1), 8, query_count), jnp.float32),
             pltpu.VMEM((ny, TAIL, per_chunk, query_count), jnp.float32),
             dma((3,)),
             dma((half_blocks + 1,)),
             dma((2,)),
             dma((2, chunks + TAIL_PARTS - 1)),
             dma,
-            dma((ny, half_blocks + 1)),
+            dma((half_blocks + 1,)),
             dma((max(1, half_blocks - 1),)),
             dma,
             dma,
-            dma((nx + 1,)),
+            dma((2,)),
             dma,
-            dma((ny, TAIL)),
+            dma,
         ],
         compiler_params=pltpu.CompilerParams(
             collective_id=0, has_side_effects=True, vmem_limit_bytes=VMEM_BYTES - 4 * query_count * block_rows

time: 44.6 us -> 44.2 us (level); the launches traced: 44.4 us -> 43.5 us
  Pallas kernels: 43.8 us -> 42.9 us
    pallas_call x1, Pallas kernels: 43.8 us -> 42.9 us  [shards(): pl.pallas_call(functools.partial(kernel, sizes), out_shape=pltpu.VMEM((qu...]
where the time goes in v3:
time: 44.2 us; the launch traced here: 43.5 us
  Pallas kernels  42.9 us (97%)
  local copies, waits for them, and re-layouts  0.63 us (1%)
    pallas_call x1, Pallas kernels, shards(): pl.pallas_call(functools.partial(kernel, sizes), out_shape=pltpu.VMEM((qu...  42.9 us

profile of v3, /device:TPU:0, one launch (start us, length us, event | category | flops | bytes accessed | tf_op | source)
XLA Modules:
  0.0 43.5 jit_solution(18244730182352300120)
XLA Ops:
  0.0 42.9 %shard_map.46 = f32[128,128]{1,0:T(8,128)S(1)} custom-call(bf16[128,8,128]{2,1,0:T(8,128)(2,1)} %queries_in.1, s32[4,128]{1,0:T(4,128)} %bitcast.2, s32[1,128]{1,0:T(1,128)} %bitcast.3, bf16[512,64,128]{2,1,0:T(8,128)(2,1)} %passages.1), custom_call_target="tpu_custom_call" | custom-call | tf_op jit(solution)/shard_map/pallas_call | solution.py:465
  42.9 0.6 %copy.6 = f32[128,128]{1,0:T(8,128)} copy(f32[128,128]{1,0:T(8,128)S(1)} %shard_map.46) | data formatting | bytes 131072

commit v4 on v3

--- a/solution.py
+++ b/solution.py
@@ -126,10 +126,10 @@
     token_ids = lax.broadcasted_iota(jnp.int32, (token_count, width), 0).astype(jnp.float32)
     tile_columns = 256
 
-    def compute(c, sides):
-        rows = len(sides) * per_chunk
+    def compute(*halves):
+        rows = len(halves) * per_chunk
         limit = []
-        for place, side in enumerate(sides):
+        for place, (side, c) in enumerate(halves):
             start = jnp.where(side == 0, low_start(c), high_start(c))
             for p in range(per_chunk):
                 tokens = x[start + p].astype(jnp.float32)
@@ -149,7 +149,7 @@
             )
             best = jnp.max(scores.reshape(rows, token_count, tile_columns), axis=1)
             best = jnp.where(any_used, best, masked_low)
-            for place, side in enumerate(sides):
+            for place, (side, c) in enumerate(halves):
                 own[side, c, :, columns] = best[place * per_chunk : (place + 1) * per_chunk]
 
     class Flow:
@@ -260,6 +260,8 @@
             device_id_type=MESH,
         )
 
+    urgent = jnp.where(gz < half_blocks, 1, 0)
+
     def pass_on(s):
         for flow in flows:
             c = s - flow.lag
@@ -286,7 +288,7 @@
             def _():
                 wait_load(group)
 
-        compute(s, (0, 1))
+        compute((urgent, s), (1 - urgent, s - 1))
         send(s)
         return carry
 
@@ -294,18 +296,18 @@
         pass_on(s)
         return carry
 
-    urgent = jnp.where(gz < half_blocks, 1, 0)
     wait_load(0)
-    compute(0, (urgent,))
+    compute((urgent, 0))
     pl.semaphore_wait(barrier, nx + ny - 2 + jnp.where(at_end, 1, 2))
     send(0)
-    compute(0, (1 - urgent,))
     lax.fori_loop(1, chunks, step, 0)
+    pass_on(chunks)
+    compute((1 - urgent, chunks - 1))
 
     @pl.when(jnp.logical_not(at_end))
     def _():
         last_lag = max(start + more * (nz - 3) for start, more in UP_LAGS + DOWN_LAGS)
-        lax.fori_loop(chunks, chunks + last_lag, drain, 0)
+        lax.fori_loop(chunks + 1, chunks + last_lag, drain, 0)
 
     for flow in flows:
         @pl.when(flow.is_last)

time: 44.2 us -> 44 us (level)
  no operation moved by 1% of the time
where the time goes in v4:
time: 44 us; the launch traced here: 43.3 us
  Pallas kernels  42.6 us (97%)
  local copies, waits for them, and re-layouts  0.63 us (1%)
    pallas_call x1, Pallas kernels, shards(): pl.pallas_call(functools.partial(kernel, sizes), out_shape=pltpu.VMEM((qu...  42.6 us

profile of v4, /device:TPU:0, one launch (start us, length us, event | category | flops | bytes accessed | tf_op | source)
XLA Modules:
  0.0 43.3 jit_solution(7474134714943786898)
XLA Ops:
  0.0 42.6 %shard_map.46 = f32[128,128]{1,0:T(8,128)S(1)} custom-call(bf16[128,8,128]{2,1,0:T(8,128)(2,1)} %queries_in.1, s32[4,128]{1,0:T(4,128)} %bitcast.2, s32[1,128]{1,0:T(1,128)} %bitcast.3, bf16[512,64,128]{2,1,0:T(8,128)(2,1)} %passages.1), custom_call_target="tpu_custom_call" | custom-call | tf_op jit(solution)/shard_map/pallas_call | solution.py:467
  42.6 0.6 %copy.6 = f32[128,128]{1,0:T(8,128)} copy(f32[128,128]{1,0:T(8,128)S(1)} %shard_map.46) | data formatting | bytes 131072

commit v5 on v4

--- a/solution.py
+++ b/solution.py
@@ -365,7 +365,11 @@
 
     far_stat = stat_copy(nx, gx, gy, 0, 1)
     beside = [lax.rem(gx + turn, nx) for turn in range(1, nx)]
-    column = [(lax.rem(gx + turn, nx), to_z) for turn in range(nx) for to_z in range(1, nz)]
+    column = [
+        (lax.rem(gx + turn, nx), to_z)
+        for to_z in reversed(range(1, nz))
+        for turn in reversed(range(nx))
+    ]
     helper = min(1, ny - 1)
     shared = (nx - 1, nx - 1 + len(column), nx - 1 + 2 * len(column))
 
@@ -406,7 +410,7 @@
             stat_copy(gx, to_x, gy, gz).start()
 
         def share(columns):
-            for to_y in (gy, 0)[:columns]:
+            for to_y in (0, gy)[2 - columns :] if columns else ():
                 for to_x, to_z in column:
                     stat_copy(gx, to_x, to_y, to_z).start()
 

time: 44 us -> 43.6 us (level)
  no operation moved by 1% of the time
where the time goes in v5:
time: 43.6 us; the launch traced here: 43.3 us
  Pallas kernels  42.6 us (98%)
  local copies, waits for them, and re-layouts  0.63 us (1%)
    pallas_call x1, Pallas kernels, shards(): pl.pallas_call(functools.partial(kernel, sizes), out_shape=pltpu.VMEM((qu...  42.6 us

profile of v5, /device:TPU:0, one launch (start us, length us, event | category | flops | bytes accessed | tf_op | source)
XLA Modules:
  0.0 43.3 jit_solution(3502534485858876585)
XLA Ops:
  0.0 42.6 %shard_map.46 = f32[128,128]{1,0:T(8,128)S(1)} custom-call(bf16[128,8,128]{2,1,0:T(8,128)(2,1)} %queries_in.1, s32[4,128]{1,0:T(4,128)} %bitcast.2, s32[1,128]{1,0:T(1,128)} %bitcast.3, bf16[512,64,128]{2,1,0:T(8,128)(2,1)} %passages.1), custom_call_target="tpu_custom_call" | custom-call | tf_op jit(solution)/shard_map/pallas_call | solution.py:471
  42.6 0.6 %copy.6 = f32[128,128]{1,0:T(8,128)} copy(f32[128,128]{1,0:T(8,128)S(1)} %shard_map.46) | data formatting | bytes 131072

commit v6 on v5

--- a/solution.py
+++ b/solution.py
@@ -10,7 +10,7 @@
 masked_low = -1e30
 MESH = pl.DeviceIdType.MESH
 UP_LAGS = ((3, 3), (2, 2))
-DOWN_LAGS = ((4, 3), (3, 2))
+DOWN_LAGS = ((4, 3), (2, 2))
 TAIL_PARTS = 2
 PEER_LAG = 3
 TAIL = 2
@@ -213,7 +213,7 @@
             for turn in reversed(range(ny)):
                 far_copy(turn, gy, c - (chunks - TAIL)).start()
 
-        for turn in range(1, ny):
+        for turn in reversed(range(1, ny)):
             peer_copy(turn, gy, piece_of(c), (c,)).start()
 
     def wait_landed(whole, sem):

time: 43.6 us -> 43.6 us (level)
  no operation moved by 1% of the time
where the time goes in v6:
time: 43.6 us; the launch traced here: 43.4 us
  Pallas kernels  42.8 us (98%)
  local copies, waits for them, and re-layouts  0.63 us (1%)
    pallas_call x1, Pallas kernels, shards(): pl.pallas_call(functools.partial(kernel, sizes), out_shape=pltpu.VMEM((qu...  42.8 us

profile of v6, /device:TPU:0, one launch (start us, length us, event | category | flops | bytes accessed | tf_op | source)
XLA Modules:
  0.0 43.4 jit_solution(7000261880105849888)
XLA Ops:
  0.0 42.8 %shard_map.46 = f32[128,128]{1,0:T(8,128)S(1)} custom-call(bf16[128,8,128]{2,1,0:T(8,128)(2,1)} %queries_in.1, s32[4,128]{1,0:T(4,128)} %bitcast.2, s32[1,128]{1,0:T(1,128)} %bitcast.3, bf16[512,64,128]{2,1,0:T(8,128)(2,1)} %passages.1), custom_call_target="tpu_custom_call" | custom-call | tf_op jit(solution)/shard_map/pallas_call | solution.py:471
  42.8 0.6 %copy.6 = f32[128,128]{1,0:T(8,128)} copy(f32[128,128]{1,0:T(8,128)S(1)} %shard_map.46) | data formatting | bytes 131072
